TPU v7x, 32 devices: a whole 2x2x4 slice. The times are simulated.
32 devices in a mesh: mb: 4 (over z), tp: 2 (over y), dp: 4 (over x, core).
Axes of the slice: x: 2, y: 2, z: 4, core: 2. Of those that a mesh axis runs over, the one named last changes fastest.
Arguments:
- hidden: bfloat16 [4, 8, 512, 7168], P('dp', 'mb', None, 'tp'), may hold values from -6 to 6
- latent: bfloat16 [4, 8, 512, 512], P('dp', 'mb', None, 'tp'), may hold values from -6 to 6
- out_grad: bfloat16 [4, 8, 512, 16384], P('dp', 'mb', None, 'tp'), may hold values from -0.059814453 to 0.059814453
- up_weight: bfloat16 [512, 16384], P(None, 'tp'), may hold values from -0.046875 to 0.046875
- mb_tokens: int32 [4, 8], P('dp'), may hold values from 128 to 512, as said below
- slot_mb: int32 [4, 8], P('dp', 'mb'), may hold values from 0 to 7, each once within a row
Outputs:
- up_grad: float32 [512, 16384], P(('mb', 'dp'), 'tp')
- running_down: float32 [4, 7168, 512], P('mb', 'tp', 'dp')
Inputs may be any that keep to these rules, and one draw needn't show every extreme that they name: `mb_tokens`: each count is a multiple of 128; in every group some microbatch has exactly 512 tokens. `slot_mb`: each row is a permutation of the microbatch numbers.
All inputs are finite; a program needn't handle non-finite values.
Results may differ from a plain program's by a relative error of at most 0.005.
Values may be sent and summed in bfloat16 or wider, within the bound.
A program may use at most 128 MiB of HBM per device.

v0:
```python
import jax
import jax.numpy as jnp
from jax import lax
from jax.sharding import PartitionSpec as P


def carried_in(part, axis, combine, identity):
    place = lax.axis_index(axis)
    gathered = lax.all_gather(part, axis)
    state = jnp.zeros_like(part) + jnp.asarray(identity, part.dtype)

    def one(lap, state):
        return combine(state, lax.dynamic_index_in_dim(gathered, lap, 0, False))

    return lax.fori_loop(0, place, one, state)


def add_terms(earlier, later):
    return earlier + later


def local(hidden, latent, out_grad, up_weight, mb_tokens, slot_mb):
    slot_count = hidden.shape[1]
    capacity = hidden.shape[2]
    micro_count = mb_tokens.shape[1]
    row_total = slot_count * capacity
    slot_ids = slot_mb[0]
    lookup = slot_ids[:, None] == jnp.arange(micro_count, dtype=jnp.int32)[None, :]
    counts = jnp.sum(jnp.where(lookup, mb_tokens[0][None, :], 0), axis=1)
    valid_rows = jnp.arange(capacity, dtype=jnp.int32)[None, :] < counts[:, None]
    masked_grads = jnp.where(valid_rows[:, :, None], out_grad[0], jnp.zeros((), out_grad.dtype))
    masked_grads = masked_grads.reshape(row_total, -1)
    factors = lax.all_gather(latent[0].reshape(row_total, -1), "tp", axis=1, tiled=True)
    partial_latent = lax.dot_general(
        masked_grads, up_weight, (((1,), (1,)), ((), ())), preferred_element_type=jnp.float32
    )
    latent_grad = lax.psum(partial_latent, "tp").astype(jnp.bfloat16)
    up_grad = lax.psum_scatter(
        lax.dot_general(
            factors, masked_grads, (((0,), (0,)), ((), ())), preferred_element_type=jnp.float32
        ),
        ("mb", "dp"),
        scatter_dimension=0,
        tiled=True,
    )
    hidden_rows = hidden[0].reshape(row_total, -1)
    down_term = lax.dot_general(
        hidden_rows, latent_grad, (((0,), (0,)), ((), ())), preferred_element_type=jnp.float32
    )
    down_share = lax.psum_scatter(down_term, "dp", scatter_dimension=1, tiled=True)
    earlier = carried_in(down_share, "mb", add_terms, jnp.zeros_like(down_share))
    running = earlier + down_share
    return (up_grad, running[None])


def solution(mesh):
    return jax.shard_map(
        local,
        mesh=mesh,
        in_specs=(
            P("dp", "mb", None, "tp"),
            P("dp", "mb", None, "tp"),
            P("dp", "mb", None, "tp"),
            P(None, "tp"),
            P("dp", None),
            P("dp", "mb"),
        ),
        out_specs=(P(("mb", "dp"), "tp"), P("mb", "tp", "dp")),
        check_vma=False,
    )
```

profile of v0, /device:TPU:0, one launch (start us, length us, event | category | flops | bytes accessed | tf_op | source)
XLA Modules:
  0.0 487.2 jit_solution(6459500900742012512)
XLA Ops:
  8.0 0.0 reduce-scatter.5.cloned.1.call-start
  8.0 0.9 fusion.1
  8.9 0.1 iota_compare_fusion
  9.0 14.0 %bitcast_select_fusion = bf16[1024,8192]{1,0:T(8,128)(2,1)} fusion(bf16[1,2,512,8192]{3,2,1,0:T(8,128)(2,1)} %param.10, pred[1024]{0:T(1024)(128)(4,1)S(1)} %lt.30), kind=kLoop, calls=%fused_computation.1 | loop fusion | flops 8388608 | bytes 33555456 | tf_op jit(solution)/shard_map/jit(_where)/select_n | solution.py:31
  23.0 14.4 %fusion.2 = f32[1024,512]{1,0:T(8,128)S(1)} fusion(bf16[1024,8192]{1,0:T(8,128)(2,1)} %bitcast_select_fusion, bf16[512,8192]{1,0:T(8,128)(2,1)} %param.11), kind=kOutput, calls=%fused_computation.9 | convolution fusion | flops 8589934592 | bytes 27262976 | tf_op jit(solution)/shard_map/dot_general | solution.py:34
  37.4 54.2 %all-reduce.1 = bf16[1024,512]{1,0:T(8,128)(2,1)S(1)} all-reduce(f32[1024,512]{1,0:T(8,128)S(1)} %fusion.2), channel_id=1, replica_groups=mesh['mb'=4,'tp'=2,'dp'=4] {'tp'}, use_global_device_ids=true, to_apply=%region_2.3 | all-reduce | flops 524288 | bytes 3145728 | tf_op jit(solution)/shard_map/psum | solution.py:37
  91.7 9.2 %convolution_bitcast_fusion.1 = f32[3584,512]{0,1:T(8,128)} fusion(bf16[1024,3584]{1,0:T(8,128)(2,1)} %bitcast.25, bf16[1024,512]{1,0:T(8,128)(2,1)S(1)} %all-reduce.1), kind=kOutput, calls=%fused_computation.3 | convolution fusion | flops 3758096384 | bytes 15728640 | tf_op jit(solution)/shard_map/dot_general | solution.py:47
  100.8 0.0 reduce-scatter.5.cloned.1.call-update
  100.8 0.0 all-gather.4.cloned.1.call-start
  100.9 0.5 all-gather.4.cloned.1.call-update
  101.4 0.0 all-gather.6.cloned.1.call-start
  101.5 65.8 %reduce-scatter.5.cloned.1.call-done = f32[3584,128]{0,1:T(8,128)} async-done(((f32[3584,512]{0,1:T(8,128)}), f32[3584,128]{0,1:T(8,128)}) %reduce-scatter.5.cloned.1.call-update) | async-done | bytes 1835024 | tf_op jit(solution)/shard_map/reduce_scatter | solution.py:50
  167.2 0.0 all-gather.6.cloned.1.call-update
  167.2 0.0 reduce-scatter.7.cloned.1.call-start
  167.3 0.0 all-gather.4.cloned.1.call-done
  167.3 16.0 %convolution_bitcast_fusion = f32[512,8192]{0,1:T(8,128)} fusion(bf16[1024,8192]{1,0:T(8,128)(2,1)} %bitcast_select_fusion, bf16[1024,512]{1,0:T(8,128)(2,1)} %all-gather.4.cloned.1.call-done), kind=kOutput, calls=%fused_computation.2 | convolution fusion | flops 8589934592 | bytes 34603008 | tf_op jit(solution)/shard_map/dot_general | solution.py:39
  183.3 17.5 %copy.21 = f32[512,8192]{1,0:T(8,128)} copy(f32[512,8192]{0,1:T(8,128)} %convolution_bitcast_fusion) | data formatting | bytes 33554432
  200.8 0.0 reduce-scatter.7.cloned.1.call-update
  200.8 98.9 %all-gather.6.cloned.1.call-done = f32[14336,128]{0,1:T(8,128)} async-done(((f32[3584,128]{0,1:T(8,128)}), f32[14336,128]{0,1:T(8,128)}) %all-gather.6.cloned.1.call-update) | async-done | bytes 7340048 | tf_op jit(solution)/shard_map/all_gather | solution.py:9
  299.7 8.6 %copy.20 = f32[14336,128]{1,0:T(8,128)} copy(f32[14336,128]{0,1:T(8,128)} %all-gather.6.cloned.1.call-done) | data formatting | bytes 14680064 | tf_op jit(solution)/shard_map/while | solution.py:15
  308.3 0.1 broadcast_in_dim.41
  308.5 1.7 copy.17
  310.2 3.0 add_bitcast_fusion
  313.2 1.7 copy.19
  314.9 164.7 %reduce-scatter.7.cloned.1.call-done = f32[32,8192]{1,0:T(8,128)} async-done(((f32[512,8192]{1,0:T(8,128)}), f32[32,8192]{1,0:T(8,128)}) %reduce-scatter.7.cloned.1.call-update) | async-done | bytes 1048592
  (2 shorter events, 0.0 us)
Async XLA Ops:
  8.0 159.2 %reduce-scatter.5.cloned.1.call-start = ((), (), s32[]{:S(2)}) async-start(), calls=%async_computation.3 | async-start | bytes 9175040 | tf_op jit(solution)/shard_map/reduce_scatter | solution.py:50
  100.8 66.5 %all-gather.4.cloned.1.call-start = ((), (), s32[]{:S(2)}) async-start(), calls=%async_computation.2 | async-start | bytes 1572864 | tf_op jit(solution)/shard_map/all_gather | solution.py:33
  101.4 198.3 %all-gather.6.cloned.1.call-start = ((), (), s32[]{:S(2)}) async-start(), calls=%async_computation.4 | async-start | bytes 9175040 | tf_op jit(solution)/shard_map/all_gather | solution.py:9
  167.2 312.4 %reduce-scatter.7.cloned.1.call-start = ((), (), s32[]{:S(2)}) async-start(), calls=%async_computation.5 | async-start | bytes 17825792
Sparse Core Ops, SparseCore 0:
  101.0 66.2 reduce-scatter.4
Sparse Core Ops, SparseCore 1:
  102.8 21.4 all-gather.3
  167.3 132.3 all-gather.5
  304.2 175.3 reduce-scatter.6
where the time goes:
time: 488 us; the launch traced here: 487 us
  waiting for transfers between devices  330 us (68%)
  blocking collectives  54.2 us (11%)
  matrix products  39.6 us (8%)
  local copies, waits for them, and re-layouts  29.6 us (6%)
  other arithmetic  18 us (4%)
  between operations  15.7 us (3%)
    unnamed x5, waiting for transfers between devices  165 us
    all_gather x1, waiting for transfers between devices, carried_in(): gathered = lax.all_gather(part, axis)  98.9 us
    reduce_scatter x1, waiting for transfers between devices, local(): lax.psum_scatter(down_term, 'dp', scatter_dimension=1, tiled=True)  65.8 us
    psum x1, blocking collectives, local(): latent_grad = lax.psum(partial_latent, 'tp').astype(jnp.bfloat16)  54.2 us
    unnamed x2, local copies, waits for them, and re-layouts  19.2 us
    dot_general x1, matrix products, local(): lax.dot_general(factors, masked_grads, (((0,), (0,)), ((), ())), preferre...  16 us
    dot_general x1, matrix products, local(): lax.dot_general(masked_grads, up_weight, (((1,), (1,)), ((), ())), prefer...  14.4 us
    select_n x1, other arithmetic, local(): jnp.where(valid_rows[:, :, None], out_grad[0], jnp.zeros((), out_grad.dty...  14 us
  transfers between devices with their start and end apart: 4, of which 3 were waited for; matrix products, arithmetic and copies ran while one was open for 10% of the time, Pallas kernels for 0%

commit v1 on v0

--- a/solution.py
+++ b/solution.py
@@ -34,7 +34,7 @@
     partial_latent = lax.dot_general(
         masked_grads, up_weight, (((1,), (1,)), ((), ())), preferred_element_type=jnp.float32
     )
-    latent_grad = lax.psum(partial_latent, "tp").astype(jnp.bfloat16)
+    latent_grad = jnp.sum(lax.all_gather(partial_latent, "tp"), axis=0).astype(jnp.bfloat16)
     up_grad = lax.psum_scatter(
         lax.dot_general(
             factors, masked_grads, (((0,), (0,)), ((), ())), preferred_element_type=jnp.float32

time: 488 us -> 520 us (1.066)
  waiting for transfers between devices: 330 us -> 414 us
  blocking collectives: 54.2 us -> 0 us
    all_gather x0 -> x1, waiting for transfers between devices: none -> 59.6 us  [local(): lax.all_gather(partial_latent, 'tp')]
    psum x1 -> x0, blocking collectives: 54.2 us -> none  [local(): latent_grad = lax.psum(partial_latent, 'tp').astype(jnp.bfloat16)]
    all_gather x1, waiting for transfers between devices: 0.02 us -> 22.6 us  [local(): lax.all_gather(latent[0].reshape(row_total, -1), 'tp', axis=1, tiled=True)]
    unnamed x5 -> x6, waiting for transfers between devices: 165 us -> 166 us
  transfers between devices with their start and end apart: 4 -> 5, of which waited for: 3 -> 5; matrix products, arithmetic and copies ran while one was open for 10% -> 9% of each run, Pallas kernels for 0% -> 0%
where the time goes in v1:
time: 520 us; the launch traced here: 519 us
  waiting for transfers between devices  414 us (80%)
  matrix products  41 us (8%)
  local copies, waits for them, and re-layouts  29.6 us (6%)
  other arithmetic  20.7 us (4%)
  between operations  13.8 us (3%)
    unnamed x6, waiting for transfers between devices  166 us
    all_gather x1, waiting for transfers between devices, carried_in(): gathered = lax.all_gather(part, axis)  100 us
    reduce_scatter x1, waiting for transfers between devices, local(): lax.psum_scatter(down_term, 'dp', scatter_dimension=1, tiled=True)  65.3 us
    all_gather x1, waiting for transfers between devices, local(): lax.all_gather(partial_latent, 'tp')  59.6 us
    all_gather x1, waiting for transfers between devices, local(): lax.all_gather(latent[0].reshape(row_total, -1), 'tp', axis=1, tiled=True)  22.6 us
    unnamed x2, local copies, waits for them, and re-layouts  19.1 us
    dot_general x1, matrix products, local(): lax.dot_general(factors, masked_grads, (((0,), (0,)), ((), ())), preferre...  16 us
    dot_general x1, matrix products, local(): lax.dot_general(masked_grads, up_weight, (((1,), (1,)), ((), ())), prefer...  15.8 us
  transfers between devices with their start and end apart: 5, of which 5 were waited for; matrix products, arithmetic and copies ran while one was open for 9% of the time, Pallas kernels for 0%

profile of v1, /device:TPU:0, one launch (start us, length us, event | category | flops | bytes accessed | tf_op | source)
XLA Modules:
  0.0 519.0 jit_solution(15517648824346551574)
XLA Ops:
  7.2 0.0 all-gather.8.cloned.1.call-start
  7.2 0.9 fusion.1
  8.1 0.1 iota_compare_fusion
  8.2 14.0 %bitcast_select_fusion = bf16[1024,8192]{1,0:T(8,128)(2,1)} fusion(bf16[1,2,512,8192]{3,2,1,0:T(8,128)(2,1)} %param.10, pred[1024]{0:T(1024)(128)(4,1)S(1)} %lt.30), kind=kLoop, calls=%fused_computation.1 | loop fusion | flops 8388608 | bytes 33555456 | tf_op jit(solution)/shard_map/jit(_where)/select_n | solution.py:31
  22.1 15.8 %fusion.2 = f32[1024,512]{1,0:T(8,128)} fusion(bf16[1024,8192]{1,0:T(8,128)(2,1)} %bitcast_select_fusion, bf16[512,8192]{1,0:T(8,128)(2,1)} %param.11), kind=kOutput, calls=%fused_computation.9 | convolution fusion | flops 8589934592 | bytes 27262976 | tf_op jit(solution)/shard_map/dot_general | solution.py:34
  38.0 0.0 all-gather.8.cloned.1.call-update
  38.0 0.0 reduce-scatter.5.cloned.1.call-start
  38.0 59.6 %all-gather.8.cloned.1.call-done = f32[2048,512]{1,0:T(8,128)} async-done(((f32[1024,512]{1,0:T(8,128)}), f32[2048,512]{1,0:T(8,128)}) %all-gather.8.cloned.1.call-update) | async-done | bytes 4194320 | tf_op jit(solution)/shard_map/all_gather | solution.py:37
  97.6 2.8 reduce_sum.19
  100.4 9.2 %convolution_bitcast_fusion.1 = f32[3584,512]{0,1:T(8,128)} fusion(bf16[1024,3584]{1,0:T(8,128)(2,1)} %bitcast.26, bf16[1024,512]{1,0:T(8,128)(2,1)S(1)} %reduce_sum.19), kind=kOutput, calls=%fused_computation.3 | convolution fusion | flops 3758096384 | bytes 15728640 | tf_op jit(solution)/shard_map/dot_general | solution.py:47
  109.5 0.0 reduce-scatter.5.cloned.1.call-update
  109.5 0.0 all-gather.6.cloned.1.call-start
  109.6 0.7 all-gather.6.cloned.1.call-update
  110.3 0.0 all-gather.10.cloned.1.call-start
  110.3 65.3 %reduce-scatter.5.cloned.1.call-done = f32[3584,128]{0,1:T(8,128)} async-done(((f32[3584,512]{0,1:T(8,128)}), f32[3584,128]{0,1:T(8,128)}) %reduce-scatter.5.cloned.1.call-update) | async-done | bytes 1835024 | tf_op jit(solution)/shard_map/reduce_scatter | solution.py:50
  175.7 0.0 all-gather.10.cloned.1.call-update
  175.7 0.2 reduce-scatter.7.cloned.1.call-start
  175.9 22.6 %all-gather.6.cloned.1.call-done = bf16[1024,512]{1,0:T(8,128)(2,1)} async-done(((bf16[1024,256]{1,0:T(8,128)(2,1)}), bf16[1024,512]{1,0:T(8,128)(2,1)}) %all-gather.6.cloned.1.call-update) | async-done | bytes 1048592 | tf_op jit(solution)/shard_map/all_gather | solution.py:33
  198.5 16.0 %convolution_bitcast_fusion = f32[512,8192]{0,1:T(8,128)} fusion(bf16[1024,8192]{1,0:T(8,128)(2,1)} %bitcast_select_fusion, bf16[1024,512]{1,0:T(8,128)(2,1)} %all-gather.6.cloned.1.call-done), kind=kOutput, calls=%fused_computation.2 | convolution fusion | flops 8589934592 | bytes 34603008 | tf_op jit(solution)/shard_map/dot_general | solution.py:39
  214.5 17.5 %copy.21 = f32[512,8192]{1,0:T(8,128)} copy(f32[512,8192]{0,1:T(8,128)} %convolution_bitcast_fusion) | data formatting | bytes 33554432
  231.9 0.0 reduce-scatter.7.cloned.1.call-update
  231.9 100.5 %all-gather.10.cloned.1.call-done = f32[14336,128]{0,1:T(8,128)} async-done(((f32[3584,128]{0,1:T(8,128)}), f32[14336,128]{0,1:T(8,128)}) %all-gather.10.cloned.1.call-update) | async-done | bytes 7340048 | tf_op jit(solution)/shard_map/all_gather | solution.py:9
  332.4 8.7 %copy.20 = f32[14336,128]{1,0:T(8,128)} copy(f32[14336,128]{0,1:T(8,128)} %all-gather.10.cloned.1.call-done) | data formatting | bytes 14680064 | tf_op jit(solution)/shard_map/while | solution.py:15
  341.1 0.1 broadcast_in_dim.41
  341.2 1.7 copy.17
  342.9 3.0 add_bitcast_fusion
  345.9 1.7 copy.19
  347.6 164.9 %reduce-scatter.7.cloned.1.call-done = f32[32,8192]{1,0:T(8,128)} async-done(((f32[512,8192]{1,0:T(8,128)}), f32[32,8192]{1,0:T(8,128)}) %reduce-scatter.7.cloned.1.call-update) | async-done | bytes 1048592
  (2 shorter events, 0.0 us)
Async XLA Ops:
  7.2 90.4 %all-gather.8.cloned.1.call-start = ((), (), s32[]{:S(2)}) async-start(), calls=%async_computation.4 | async-start | bytes 6291456 | tf_op jit(solution)/shard_map/all_gather | solution.py:37
  38.0 137.7 %reduce-scatter.5.cloned.1.call-start = ((), (), s32[]{:S(2)}) async-start(), calls=%async_computation.3 | async-start | bytes 9175040 | tf_op jit(solution)/shard_map/reduce_scatter | solution.py:50
  109.5 88.9 %all-gather.6.cloned.1.call-start = ((), (), s32[]{:S(2)}) async-start(), calls=%async_computation.2 | async-start | bytes 1572864 | tf_op jit(solution)/shard_map/all_gather | solution.py:33
  110.3 222.1 %all-gather.10.cloned.1.call-start = ((), (), s32[]{:S(2)}) async-start(), calls=%async_computation.5 | async-start | bytes 9175040 | tf_op jit(solution)/shard_map/all_gather | solution.py:9
  175.7 336.8 %reduce-scatter.7.cloned.1.call-start = ((), (), s32[]{:S(2)}) async-start(), calls=%async_computation.6 | async-start | bytes 17825792
Sparse Core Ops, SparseCore 0:
  38.1 59.4 all-gather.7
  109.7 65.9 reduce-scatter.4
  177.2 21.2 all-gather.5
  199.9 132.4 all-gather.9
  336.9 175.5 reduce-scatter.6
